TPU v7x, 32 devices: a whole 2x2x4 slice. The times are simulated.
32 devices in a mesh: dp: 4 (over z), seq: 4 (over y, core), tp: 2 (over x).
Axes of the slice: x: 2, y: 2, z: 4, core: 2. Of those that a mesh axis runs over, the one named last changes fastest.
Arguments:
- queries: bfloat16 [8192, 1024], P(('dp', 'seq'), 'tp'), parts along dimension 0, may hold values from -181 to 181
- rotated_key_states: bfloat16 [8192, 256], P(('dp', 'seq'), 'tp'), parts along dimension 0, may hold values from -6.1 to 6.1
- value_state_vectors: bfloat16 [8192, 256], P(('dp', 'seq'), 'tp'), parts along dimension 0, may hold values from -6 to 6
- out_weight: bfloat16 [1024, 8192], P('tp'), may hold values from -0.3125 to 0.3125
- residual: bfloat16 [8192, 8192], P(('dp', 'seq', 'tp')), parts along dimension 0, may hold values from -0.75 to 0.75
- norm_gain: bfloat16 [8192], replicated, may hold values from 0.099609375 to 2
Outputs:
- new_residual: bfloat16 [8192, 8192], P(('dp', 'seq', 'tp')), parts along dimension 0
- next_input: bfloat16 [8192, 8192], P(('dp', 'seq', 'tp')), parts along dimension 0
There are 4 independent parts, one for each index of `dp`. A program takes and returns all parts, laid end to end along the dimension named above; an argument that names none is the same for every part. Nothing has to cross between parts.
All inputs are finite; a program needn't handle non-finite values.
Results may differ from a plain program's by a relative error of at most 0.025.
Values may be sent and summed in bfloat16 or wider, within the bound.
A program may use at most 192 MiB of HBM per device.

v0:
```python
import jax
import jax.numpy as jnp
from jax import lax
from jax.sharding import PartitionSpec as P

D = 8192
HEAD_SIZE = 128


softness = 0.9
scale_floor = 256.0
neg_large = -1e30


def soft_grid(values):
    return values - softness * jnp.sin(jnp.pi * values) / jnp.pi


def fake_quant(blocks, block_axis, peak):
    block_max = jnp.max(jnp.abs(blocks), axis=block_axis, keepdims=True)
    tensor_scale = peak / (6.0 * 448.0)
    block_scale = jnp.maximum(block_max / (6.0 * tensor_scale), scale_floor).astype(jnp.bfloat16)
    block_scale = lax.optimization_barrier(block_scale).astype(jnp.float32)
    spacing = block_scale * tensor_scale
    payload = soft_grid(blocks / spacing).astype(jnp.bfloat16)
    payload = lax.optimization_barrier(payload).astype(jnp.float32)
    return (payload * spacing).astype(jnp.bfloat16)


def attend_piece(attn_state, q_grouped, kv_piece, query_pos, causal_piece):
    running_max, running_total, running_sum = attn_state
    kv_heads = q_grouped.shape[1]
    piece_rows = kv_piece.shape[1]
    keys_split = kv_piece[0].reshape(piece_rows, kv_heads, HEAD_SIZE)
    values_split = kv_piece[1].reshape(piece_rows, kv_heads, HEAD_SIZE)
    scores = jnp.einsum(
        "tkgd,skd->kgts", q_grouped, keys_split, preferred_element_type=jnp.float32
    ) * HEAD_SIZE ** (-0.5)
    if causal_piece:
        key_pos = lax.broadcasted_iota(jnp.int32, (1, piece_rows), 1)
        allowed = query_pos[:, None] >= key_pos
        masked = jnp.where(allowed, scores, neg_large)
        new_max = jnp.maximum(running_max, jnp.max(masked, axis=3))
        weights = jnp.where(allowed, jnp.exp(masked - new_max[..., None]), 0.0)
    else:
        new_max = jnp.maximum(running_max, jnp.max(scores, axis=3))
        weights = jnp.exp(scores - new_max[..., None])
    shrink_factor = jnp.exp(running_max - new_max)
    running_total = running_total * shrink_factor + jnp.sum(weights, axis=3)
    running_sum = running_sum * shrink_factor[..., None] + jnp.einsum(
        "kgts,skd->kgtd",
        weights.astype(jnp.bfloat16),
        values_split,
        preferred_element_type=jnp.float32,
    )
    return (new_max, running_total, running_sum)


def local(queries, rotated_key_states, value_state_vectors, out_weight, residual, norm_gain):
    token_count = queries.shape[0]
    kv_heads = rotated_key_states.shape[1] // HEAD_SIZE
    grouped_heads = queries.shape[1] // HEAD_SIZE // kv_heads
    seq_rank = lax.axis_index("seq")
    q_grouped = queries.reshape(token_count, kv_heads, grouped_heads, HEAD_SIZE)
    first_query = seq_rank * token_count
    last_query = first_query + token_count - 1
    query_pos = first_query + lax.broadcasted_iota(jnp.int32, (token_count,), 0)
    kv_own = jnp.stack((rotated_key_states, value_state_vectors))
    start_state = (
        jnp.full((kv_heads, grouped_heads, token_count), neg_large, jnp.float32),
        jnp.zeros((kv_heads, grouped_heads, token_count), jnp.float32),
        jnp.zeros((kv_heads, grouped_heads, token_count, HEAD_SIZE), jnp.float32),
    )

    def fold_piece(attn_state, kv_piece, first_row):
        piece_rows = kv_piece.shape[1]

        def before_queries(state_in):
            return attend_piece(state_in, q_grouped, kv_piece, query_pos, False)

        def across_queries(state_in):
            return attend_piece(state_in, q_grouped, kv_piece, query_pos, True)

        def after_queries(state_in):
            return state_in

        branch_index = jnp.where(
            first_row + piece_rows <= first_query, 0, jnp.where(first_row <= last_query, 1, 2)
        ).astype(jnp.int32)
        return lax.switch(branch_index, [before_queries, across_queries, after_queries], attn_state)

    final_state = fold_piece(
        start_state, lax.all_gather(kv_own, "seq", axis=1, tiled=True), jnp.int32(0)
    )
    attended = (final_state[2] / final_state[1][..., None]).astype(jnp.bfloat16)
    features = attended.shape[0] * attended.shape[1] * HEAD_SIZE
    act_t = attended.transpose(0, 1, 3, 2).reshape(features, token_count).astype(jnp.float32)
    weight_f = out_weight.astype(jnp.float32)
    act_local = jnp.max(jnp.abs(act_t))
    weight_local = jnp.max(jnp.abs(weight_f))
    weight_peak = lax.pmax(weight_local, "tp")
    act_peak = lax.pmax(act_local, ("seq", "tp"))
    act_q = fake_quant(act_t.reshape(features // 16, 16, token_count), 1, act_peak).reshape(
        features, token_count
    )
    weight_q = fake_quant(weight_f.reshape(features // 16, 16, D), 1, weight_peak).reshape(
        features, D
    )
    share_rows = token_count // lax.axis_size("tp")
    projected = lax.psum_scatter(
        lax.dot_general(
            act_q, weight_q, (((0,), (0,)), ((), ())), preferred_element_type=jnp.float32
        ).astype(jnp.bfloat16),
        "tp",
        scatter_dimension=0,
        tiled=True,
    ).astype(jnp.float32)
    hidden_sum = residual.astype(jnp.float32) + projected
    new_residual = hidden_sum.astype(jnp.bfloat16)
    mean_square = jnp.mean(hidden_sum * hidden_sum, axis=1, keepdims=True)
    normed = hidden_sum * lax.rsqrt(mean_square + 1e-05) * norm_gain.astype(jnp.float32)
    norm_peak = lax.pmax(jnp.max(jnp.abs(normed)), ("seq", "tp"))
    next_input = fake_quant(normed.reshape(share_rows, D // 16, 16), 2, norm_peak).reshape(
        share_rows, D
    )
    return (new_residual, next_input)


def solution(mesh):
    in_specs = (
        P(("dp", "seq"), "tp"),
        P(("dp", "seq"), "tp"),
        P(("dp", "seq"), "tp"),
        P("tp", None),
        P(("dp", "seq", "tp"), None),
        P(),
    )
    out_specs = (P(("dp", "seq", "tp"), None), P(("dp", "seq", "tp"), None))
    return jax.shard_map(local, mesh=mesh, in_specs=in_specs, out_specs=out_specs, check_vma=False)
```

profile of v0, /device:TPU:0, one launch (start us, length us, event | category | flops | bytes accessed | tf_op | source)
XLA Modules:
  0.0 346.3 jit_solution(3365243596812530986)
XLA Ops:
  7.2 1.7 pad_maximum_fusion
  9.0 12.6 %abs_reduce_fusion.1 = (f32[32,8192]{1,0:T(8,128)S(1)}, f32[512,8192]{1,0:T(8,128)}) fusion(bf16[512,8192]{1,0:T(8,128)(2,1)} %param.12), kind=kLoop, calls=%fused_computation.48 | loop fusion | flops 12320768 | bytes 26214400 | tf_op jit(solution)/shard_map/reduce_max | solution.py:20
  21.5 5.2 %abs_reduce_fusion = f32[]{:T(128)} fusion(bf16[512,8192]{1,0:T(8,128)(2,1)} %param.12), kind=kLoop, calls=%fused_computation.47 | loop fusion | flops 12582911 | bytes 8388612 | tf_op jit(solution)/shard_map/reduce_max | solution.py:100
  27.0 6.7 %pmax.22 = f32[]{:T(128)} all-reduce(f32[]{:T(128)} %abs_reduce_fusion), channel_id=1, replica_groups=mesh['dp'=4,'seq'=4,'tp'=2] {'tp'}, use_global_device_ids=true, to_apply=%region_12.13 | all-reduce | flops 1 | bytes 8 | tf_op jit(solution)/shard_map/pmax | solution.py:101
  35.2 63.5 %subtract_convert_fusion = bf16[32,16,8192]{2,0,1:T(8,128)(2,1)} fusion(f32[32,16,8192]{2,1,0:T(8,128)} %bitcast.118, f32[32,8192]{1,0:T(8,128)S(1)} %multiply_bitcast_fusion), kind=kLoop, calls=%fused_computation.46 | loop fusion | flops 20971520 | bytes 26214400 | tf_op jit(solution)/shard_map/convert_element_type | solution.py:25
  98.6 8.9 %multiply_convert_fusion = bf16[32,16,8192]{2,0,1:T(8,128)(2,1)} fusion(bf16[32,16,8192]{2,0,1:T(8,128)(2,1)} %subtract_convert_fusion, f32[32,8192]{1,0:T(8,128)S(1)} %multiply_bitcast_fusion), kind=kLoop, calls=%fused_computation.45 | loop fusion | flops 12582912 | bytes 17825792 | tf_op jit(solution)/shard_map/convert_element_type | solution.py:27
  107.5 14.9 %conditional.1 = (f32[1,4,512]{2,1,0:T(4,128)S(1)}, f32[1,4,512,128]{2,3,1,0:T(8,128)S(1)}) conditional(s32[]{:T(128)} %clamp.3, (bf16[2,2048,128]{2,1,0:T(8,128)(2,1)}, bf16[512,1,4,128]{0,3,2,1:T(8,128)(2,1)S(1)}) %tuple.45, (s32[]{:T(128)}, s32[512]{0:T(512)S(1)}, bf16[2,2048,128]{2,1,0:T(8,128)(2,1)}, ...), branch_computations={%region_0.3_spmd, %region_3.6_spmd, %region_6.7_spmd} | conditional | flops 2203326976 | bytes 63535152 | solution.py:90
  108.3 4.1 %fusion.19 = (f32[4,512]{1,0:T(4,128)S(1)}, f32[2048,512,4]{1,0,2:T(8,128)S(1)}) fusion(pred[512,2048]{0,1:T(8,128)(4,1)S(1)} %iota_compare_fusion, bf16[512,1,4,128]{0,3,2,1:T(8,128)(2,1)S(1)} %get-tuple-element.31, bf16[2,2048,128]{2,1,0:T(8,128)(2,1)} %get-tuple-element.18), kind=kOutput, calls=%fused_computation.21 | convolution fusion | flops 1086322688 | bytes 18882560 | tf_op jit(solution)/shard_map/cond/branch_1_fun/tkgd,skd->kgts/dot_general | solution.py:36
  112.5 4.4 %fusion.21 = f32[4,512]{1,0:T(4,128)S(1)} fusion(f32[2048,512,4]{1,0,2:T(8,128)S(1)} %get-tuple-element.48, f32[4,512]{1,0:T(4,128)S(1)} %broadcast_maximum_fusion.1, pred[512,2048]{0,1:T(8,128)(4,1)S(1)} %iota_compare_fusion), kind=kLoop, calls=%fused_computation.23 | loop fusion | flops 20969472 | bytes 17842176 | tf_op jit(solution)/shard_map/cond/branch_1_fun/reduce_sum | solution.py:49
  116.9 5.1 %fusion.29 = f32[1,4,512,128]{3,2,1,0:T(8,128)S(1)} fusion(f32[2048,512,4]{1,0,2:T(8,128)S(1)} %get-tuple-element.48, f32[4,512]{1,0:T(4,128)S(1)} %broadcast_maximum_fusion.1, pred[512,2048]{0,1:T(8,128)(4,1)S(1)} %iota_compare_fusion, bf16[2,2048,128]{2,1,0:T(8,128)(2,1)S(1)} %copy-done.5, f32[4,512]{1,0:T(4,128)S(1)} %get-tuple-element.45), kind=kOutput, calls=%fused_computation.29 | convolution fusion | flops 1094975488 | bytes 19415040 | tf_op jit(solution)/shard_map/cond/branch_1_fun/kgts,skd->kgtd/dot_general | solution.py:50
  123.1 14.5 %pmax.21 = f32[]{:T(128)} all-reduce(f32[]{:T(128)} %get-tuple-element.37), channel_id=1, replica_groups=mesh['dp'=4,'seq'=4,'tp'=2] {'seq','tp'}, use_global_device_ids=true, to_apply=%region_9.10 | all-reduce | flops 1 | bytes 8 | tf_op jit(solution)/shard_map/pmax | solution.py:102
  139.2 3.7 %subtract_convert_fusion.2 = bf16[32,16,512]{2,1,0:T(8,128)(2,1)S(1)} fusion(f32[32,16,512]{2,1,0:T(8,128)S(1)} %bitcast.121, f32[32,512]{1,0:T(8,128)S(1)} %multiply_bitcast_fusion.2), kind=kLoop, calls=%fused_computation.61 | loop fusion | flops 1310720 | bytes 1638400 | tf_op jit(solution)/shard_map/convert_element_type | solution.py:25
  142.9 16.7 %bitcast_convert_fusion = bf16[512,8192]{1,0:T(8,128)(2,1)} fusion(bf16[32,16,8192]{2,0,1:T(8,128)(2,1)} %multiply_convert_fusion, bf16[32,16,512]{2,1,0:T(8,128)(2,1)S(1)} %subtract_convert_fusion.2, f32[32,512]{1,0:T(8,128)S(1)} %multiply_bitcast_fusion.2), kind=kOutput, calls=%fused_computation.43 | convolution fusion | flops 4299948032 | bytes 17367040 | tf_op jit(solution)/shard_map/dot_general | solution.py:111
  160.3 99.4 %reduce-scatter.2.cloned.1.call-done = bf16[256,8192]{1,0:T(8,128)(2,1)} async-done(((bf16[512,8192]{1,0:T(8,128)(2,1)}), bf16[256,8192]{1,0:T(8,128)(2,1)}) %reduce-scatter.2.cloned.1.call-update) | async-done | bytes 4194320 | tf_op jit(solution)/shard_map/reduce_scatter | solution.py:110
  259.7 5.0 %multiply_reduce_fusion = f32[256]{0:T(256)S(1)} fusion(bf16[256,8192]{1,0:T(8,128)(2,1)} %reduce-scatter.2.cloned.1.call-done, bf16[256,8192]{1,0:T(8,128)(2,1)} %param.13), kind=kLoop, calls=%fused_computation.55 | loop fusion | flops 10485504 | bytes 8389632 | tf_op jit(solution)/shard_map/reduce_sum | solution.py:120
  264.7 0.9 copy-done.2
  265.6 6.2 %abs_reduce_fusion.2 = (f32[]{:T(128)}, f32[256,8192]{1,0:T(8,128)}, bf16[256,8192]{1,0:T(8,128)(2,1)}) fusion(f32[8192]{0:T(1024)S(1)} %convert_element_type.145, f32[256]{0:T(256)S(1)} %add_rsqrt_fusion, bf16[256,8192]{1,0:T(8,128)(2,1)S(1)} %copy-done.2, bf16[256,8192]{1,0:T(8,128)(2,1)S(1)} %copy-done.1), kind=kLoop, calls=%fused_computation.52 | loop fusion | flops 16777215 | bytes 21005316 | tf_op jit(solution)/shard_map/reduce_max | solution.py:122
  271.8 13.2 %pmax.23 = f32[]{:T(128)} all-reduce(f32[]{:T(128)} %get-tuple-element.35), channel_id=1, replica_groups=mesh['dp'=4,'seq'=4,'tp'=2] {'seq','tp'}, use_global_device_ids=true, to_apply=%region_17.18 | all-reduce | flops 1 | bytes 8 | tf_op jit(solution)/shard_map/pmax | solution.py:122
  286.3 9.0 %copy.19 = f32[256,8192]{0,1:T(8,128)} copy(f32[256,8192]{1,0:T(8,128)} %get-tuple-element.36) | data formatting | bytes 16777216 | tf_op jit(solution)/shard_map/mul | solution.py:121
  295.4 4.8 %abs_reduce_fusion.3 = f32[256,512]{0,1:T(8,128)S(1)} fusion(f32[256,8192]{0,1:T(8,128)} %copy.19), kind=kLoop, calls=%fused_computation.53 | loop fusion | flops 4063232 | bytes 8912896 | tf_op jit(solution)/shard_map/reduce_max | solution.py:20
  300.3 0.9 copy-done
  301.1 29.0 %subtract_convert_fusion.1 = bf16[256,512,16]{0,2,1:T(8,128)(2,1)S(1)} fusion(f32[256,512]{0,1:T(8,128)S(1)} %multiply_bitcast_fusion.1, f32[256,8192]{0,1:T(8,128)S(1)} %copy-done), kind=kLoop, calls=%fused_computation.51 | loop fusion | flops 10485760 | bytes 13107200 | tf_op jit(solution)/shard_map/convert_element_type | solution.py:25
  330.1 3.1 multiply_convert_fusion.1
  333.2 6.3 %copy.20 = bf16[256,8192]{1,0:T(8,128)(2,1)} copy(bf16[256,8192]{0,1:T(8,128)(2,1)} %bitcast.119) | data formatting | bytes 8388608
  (32 shorter events, 3.5 us)
Async XLA Ops:
  7.2 100.3 %all-gather.2.cloned.1.call-start = ((), (), s32[]{:S(2)}) async-start(), calls=%async_computation.1 | async-start | bytes 1310720 | tf_op jit(solution)/shard_map/all_gather | solution.py:93
  8.9 250.8 %reduce-scatter.2.cloned.1.call-start = ((), (), s32[]{:S(2)}) async-start(), calls=%async_computation.2 | async-start | bytes 12582912 | tf_op jit(solution)/shard_map/reduce_scatter | solution.py:110
  21.5 5.2 %copy-start.3 = (bf16[512,512]{1,0:T(8,128)(2,1)S(1)}, bf16[512,512]{1,0:T(8,128)(2,1)}, u32[]{:S(2)}) copy-start(bf16[512,512]{1,0:T(8,128)(2,1)} %param.9) | copy-start | bytes 1572868
  112.4 4.4 %copy-start.5 = (bf16[2,2048,128]{2,1,0:T(8,128)(2,1)S(1)}, bf16[2,2048,128]{2,1,0:T(8,128)(2,1)}, u32[]{:S(2)}) copy-start(bf16[2,2048,128]{2,1,0:T(8,128)(2,1)} %get-tuple-element.18) | copy-start | bytes 3145732 | tf_op jit(solution)/shard_map/cond
  159.6 0.7 copy-start.6
  259.7 5.1 %copy-start.1 = (bf16[256,8192]{1,0:T(8,128)(2,1)S(1)}, bf16[256,8192]{1,0:T(8,128)(2,1)}, u32[]{:S(2)}) copy-start(bf16[256,8192]{1,0:T(8,128)(2,1)} %param.13) | copy-start | bytes 12582916
  259.7 5.9 %copy-start.2 = (bf16[256,8192]{1,0:T(8,128)(2,1)S(1)}, bf16[256,8192]{1,0:T(8,128)(2,1)}, u32[]{:S(2)}) copy-start(bf16[256,8192]{1,0:T(8,128)(2,1)} %reduce-scatter.2.cloned.1.call-done) | copy-start | bytes 12582916
  295.4 5.8 %copy-start = (f32[256,8192]{0,1:T(8,128)S(1)}, f32[256,8192]{0,1:T(8,128)}, u32[]{:S(2)}) copy-start(f32[256,8192]{0,1:T(8,128)} %copy.19) | copy-start | bytes 25165828
Sparse Core Ops, SparseCore 0:
  10.1 19.4 all-gather.1
  159.8 99.8 reduce-scatter.1
where the time goes:
time: 347 us; the launch traced here: 346 us
  other arithmetic  150 us (43%)
  waiting for transfers between devices  99.4 us (29%)
  blocking collectives  34.5 us (10%)
  matrix products  26 us (7%)
  local copies, waits for them, and re-layouts  18.3 us (5%)
  between operations  18 us (5%)
    reduce_scatter x1, waiting for transfers between devices, local(): lax.psum_scatter(lax.dot_general(act_q, weight_q, (((0,), (0,)), ((), ())...  99.4 us
    convert_element_type x3, other arithmetic, fake_quant(): payload = soft_grid(blocks / spacing).astype(jnp.bfloat16)  96.1 us
    reduce_max x3, other arithmetic, fake_quant(): block_max = jnp.max(jnp.abs(blocks), axis=block_axis, keepdims=True)  17.5 us
    dot_general x1, matrix products, local(): lax.dot_general(act_q, weight_q, (((0,), (0,)), ((), ())), preferred_elem...  16.7 us
    pmax x1, blocking collectives, local(): act_peak = lax.pmax(act_local, ('seq', 'tp'))  14.5 us
    pmax x1, blocking collectives, local(): norm_peak = lax.pmax(jnp.max(jnp.abs(normed)), ('seq', 'tp'))  13.2 us
    convert_element_type x2, other arithmetic, fake_quant(): return (payload * spacing).astype(jnp.bfloat16)  11.9 us
    mul x1, local copies, waits for them, and re-layouts, local(): hidden_sum * lax.rsqrt(mean_square + 1e-05) * norm_gain.astype(jnp.float32)  9.02 us
  transfers between devices with their start and end apart: 2, of which 1 were waited for; matrix products, arithmetic and copies ran while one was open for 26% of the time, Pallas kernels for 0%

commit v1 on v0

v1 whole, which is shorter than its diff:
```python
import functools

import jax
import jax.numpy as jnp
from jax import lax
from jax.experimental import pallas as pl
from jax.experimental.pallas import tpu as pltpu
from jax.sharding import PartitionSpec as P

HEAD_SIZE = 128
BLOCK = 16
softness = 0.9
scale_floor = 256.0
neg_large = -1e30
ROUND_BIG = 12582912.0
Q_COEFFS = (0.8999997814, -0.5804296733, 0.1500389216, -0.0212977078, 0.0016888914)


def soft_grid(u):
    turns = (u * 0.5 + ROUND_BIG) - ROUND_BIG
    t = u - (turns + turns)
    z = t * t
    q = jnp.float32(Q_COEFFS[-1])
    for c in Q_COEFFS[-2::-1]:
        q = q * z + jnp.float32(c)
    return u - (t - t * z) * q


def spacing_of(block_max, peak):
    tensor_scale = peak / (6.0 * 448.0)
    inv = 1.0 / (6.0 * tensor_scale)
    scale = jnp.maximum(block_max * inv, scale_floor).astype(jnp.bfloat16)
    return scale, tensor_scale


def quant_rows(x, peak):
    rows, cols = x.shape
    xb = x.reshape(rows // BLOCK, BLOCK, cols)
    block_max = jnp.max(jnp.abs(xb), axis=1, keepdims=True)
    scale, tensor_scale = spacing_of(block_max, peak)
    spacing = scale.astype(jnp.float32) * tensor_scale
    payload = soft_grid(xb * (1.0 / spacing)).astype(jnp.bfloat16).astype(jnp.float32)
    return (payload * spacing).reshape(rows, cols)


def quant_kernel(peak_ref, w_ref, out_ref, *, unroll):
    peak = peak_ref[0, 0]
    rows = w_ref.shape[0]

    def step(i, carry):
        sl = pl.ds(pl.multiple_of(i * BLOCK, BLOCK), BLOCK)
        out_ref[sl, :] = quant_rows(w_ref[sl, :].astype(jnp.float32), peak).astype(jnp.bfloat16)
        return carry

    lax.fori_loop(0, rows // BLOCK, step, 0, unroll=unroll)


def quant_weight(w, peak, width):
    rows, cols = w.shape
    return pl.pallas_call(
        functools.partial(quant_kernel, unroll=4),
        grid=(cols // width,),
        in_specs=[
            pl.BlockSpec(memory_space=pltpu.SMEM),
            pl.BlockSpec((rows, width), lambda i: (0, i)),
        ],
        out_specs=pl.BlockSpec((rows, width), lambda i: (0, i)),
        out_shape=jax.ShapeDtypeStruct((rows, cols), jnp.bfloat16),
        cost_estimate=pl.CostEstimate(
            flops=40 * rows * cols, bytes_accessed=4 * rows * cols, transcendentals=0
        ),
        name="quant_weight",
    )(peak, w)


def project_kernel(*refs, n_tp, n_feat):
    peak_ref, act_refs = refs[0], refs[1 : 1 + n_tp]
    own_ref, peer_ref, res_ref, gain_ref = refs[1 + n_tp : 5 + n_tp]
    new_ref, hid_ref, rstd_ref, top_ref = refs[5 + n_tp : 9 + n_tp]
    act_q, square_sum, row_top = refs[9 + n_tp :]
    step_id = pl.program_id(0)

    @pl.when(step_id == 0)
    def _():
        peak = peak_ref[0, 0]
        square_sum[...] = jnp.zeros_like(square_sum)
        row_top[...] = jnp.zeros_like(row_top)
        for k in range(n_tp):
            for lo in range(0, n_feat, 128):
                x = act_refs[k][lo : lo + 128, :].astype(jnp.float32)
                act_q[k, :, lo : lo + 128] = quant_rows(x, peak).T.astype(jnp.bfloat16)

    hidden = res_ref[...].astype(jnp.float32)
    for k in range(n_tp):
        w = own_ref[...] if k == 0 else peer_ref[0, k - 1]
        part = jnp.dot(act_q[k], w, preferred_element_type=jnp.float32)
        hidden = hidden + part.astype(jnp.bfloat16).astype(jnp.float32)
    new_ref[...] = hidden.astype(jnp.bfloat16)
    hid_ref[...] = hidden
    sq = square_sum[...]
    top = row_top[...]
    scaled = jnp.abs(hidden * gain_ref[...])
    for lo in range(0, hidden.shape[1], 128):
        part = hidden[:, lo : lo + 128]
        sq = sq + part * part
        top = jnp.maximum(top, scaled[:, lo : lo + 128])
    square_sum[...] = sq
    row_top[...] = top

    @pl.when(step_id == pl.num_programs(0) - 1)
    def _():
        width = hidden.shape[1] * pl.num_programs(0)
        mean_square = jnp.sum(square_sum[...], axis=1, keepdims=True) / width
        rstd = lax.rsqrt(mean_square + 1e-05)
        rstd_ref[...] = jnp.broadcast_to(rstd, rstd_ref.shape)
        top_all = jnp.max(jnp.max(row_top[...], axis=1, keepdims=True) * rstd)
        top_ref[...] = jnp.full(top_ref.shape, top_all, jnp.float32)


def project(peak, acts, w_own, w_peer, residual, gain):
    n_tp = len(acts)
    n_feat, tokens = acts[0].shape
    steps, _, _, width = w_peer.shape
    d = residual.shape[1]
    column = pl.BlockSpec((tokens, width), lambda i: (0, i))
    whole = pl.BlockSpec((tokens, 128), lambda i: (0, 0))
    return pl.pallas_call(
        functools.partial(project_kernel, n_tp=n_tp, n_feat=n_feat),
        grid=(steps,),
        in_specs=[pl.BlockSpec(memory_space=pltpu.SMEM)]
        + [pl.BlockSpec((n_feat, tokens), lambda i: (0, 0))] * n_tp
        + [
            pl.BlockSpec((n_feat, width), lambda i: (0, i)),
            pl.BlockSpec((1, n_tp - 1, n_feat, width), lambda i: (i, 0, 0, 0)),
            column,
            pl.BlockSpec((1, width), lambda i: (0, i)),
        ],
        out_specs=[column, column, whole, pl.BlockSpec((8, 128), lambda i: (0, 0))],
        out_shape=[
            jax.ShapeDtypeStruct((tokens, d), jnp.bfloat16),
            jax.ShapeDtypeStruct((tokens, d), jnp.float32),
            jax.ShapeDtypeStruct((tokens, 128), jnp.float32),
            jax.ShapeDtypeStruct((8, 128), jnp.float32),
        ],
        scratch_shapes=[
            pltpu.VMEM((n_tp, tokens, n_feat), jnp.bfloat16),
            pltpu.VMEM((tokens, 128), jnp.float32),
            pltpu.VMEM((tokens, 128), jnp.float32),
        ],
        cost_estimate=pl.CostEstimate(
            flops=2 * n_tp * n_feat * tokens * d, bytes_accessed=2 * n_tp * n_feat * d, transcendentals=0
        ),
        name="project",
    )(peak, *acts, w_own, w_peer, residual, gain)


def final_kernel(peak_ref, hid_ref, rstd_ref, gain_ref, out_ref):
    peak = peak_ref[0, 0]
    rows = hid_ref.shape[0]
    cols = hid_ref.shape[1]
    src = lax.broadcasted_iota(jnp.int32, (128, 128), 0)
    dst = lax.broadcasted_iota(jnp.int32, (128, 128), 1)
    spread = jnp.where(src == (dst // BLOCK) * BLOCK + BLOCK - 1, 1.0, 0.0).astype(jnp.bfloat16)
    rstd = rstd_ref[...]
    for lo in range(0, cols, 128):
        x = hid_ref[:, lo : lo + 128] * rstd * gain_ref[:, lo : lo + 128]
        m = jnp.abs(x)
        for s in (1, 2, 4, 8):
            m = jnp.maximum(m, pltpu.roll(m, s, 1))
        scale, tensor_scale = spacing_of(m, peak)
        scale = jnp.dot(scale, spread, preferred_element_type=jnp.float32)
        spacing = scale * tensor_scale
        payload = soft_grid(x / spacing).astype(jnp.bfloat16).astype(jnp.float32)
        out_ref[:, lo : lo + 128] = (payload * spacing).astype(jnp.bfloat16)


def final_quant(peak, hidden, rstd, gain):
    tokens, d = hidden.shape
    width = 1024
    rows = min(64, tokens)
    column = pl.BlockSpec((rows, width), lambda i, j: (i, j))
    return pl.pallas_call(
        final_kernel,
        grid=(tokens // rows, d // width),
        in_specs=[
            pl.BlockSpec(memory_space=pltpu.SMEM),
            column,
            pl.BlockSpec((rows, 128), lambda i, j: (i, 0)),
            pl.BlockSpec((1, width), lambda i, j: (0, j)),
        ],
        out_specs=column,
        out_shape=jax.ShapeDtypeStruct((tokens, d), jnp.bfloat16),
        name="final_quant",
    )(peak, hidden, rstd, gain)


def attend(queries, keys, values, first_query):
    token_count = queries.shape[0]
    kv_heads = keys.shape[1] // HEAD_SIZE
    grouped = queries.shape[1] // HEAD_SIZE // kv_heads
    q = queries.reshape(token_count, kv_heads, grouped, HEAD_SIZE)
    k = keys.reshape(-1, kv_heads, HEAD_SIZE)
    v = values.reshape(-1, kv_heads, HEAD_SIZE)
    scores = jnp.einsum("tkgd,skd->kgts", q, k, preferred_element_type=jnp.float32)
    scores = scores * HEAD_SIZE ** (-0.5)
    query_pos = first_query + lax.broadcasted_iota(jnp.int32, (token_count, 1), 0)
    key_pos = lax.broadcasted_iota(jnp.int32, (1, k.shape[0]), 1)
    allowed = query_pos >= key_pos
    masked = jnp.where(allowed, scores, neg_large)
    top = jnp.max(masked, axis=3, keepdims=True)
    weights = jnp.where(allowed, jnp.exp(masked - top), 0.0)
    total = jnp.sum(weights, axis=3)
    summed = jnp.einsum(
        "kgts,skd->kgtd", weights.astype(jnp.bfloat16), v, preferred_element_type=jnp.float32
    )
    attended = (summed / total[..., None]).astype(jnp.bfloat16)
    return attended.transpose(0, 1, 3, 2).reshape(-1, token_count)


def local(queries, keys, values, out_weight, residual, norm_gain):
    token_count = queries.shape[0]
    n_tp = lax.axis_size("tp")
    tp_rank = lax.axis_index("tp")
    slabs = lax.axis_size("dp") * lax.axis_size("seq")
    d = out_weight.shape[1]
    width = d // slabs
    kv = lax.all_gather(jnp.stack((keys, values)), "seq", axis=1, tiled=True)

    weight_top = jnp.max(jnp.abs(out_weight)).astype(jnp.float32)
    weight_peak = lax.pmax(weight_top, "tp").reshape(1, 1)
    slab_id = lax.axis_index("dp") * lax.axis_size("seq") + lax.axis_index("seq")
    slab = lax.dynamic_slice_in_dim(out_weight, slab_id * width, width, axis=1)
    slab_q = quant_weight(slab, weight_peak, width)
    shifts = [[(i, (i + k) % n_tp) for i in range(n_tp)] for k in range(1, n_tp)]
    from_peers = jnp.stack([lax.ppermute(slab_q, "tp", ring) for ring in shifts])
    w_peer = lax.all_gather(from_peers, ("dp", "seq"), axis=0)
    w_own = quant_weight(out_weight, weight_peak, width)

    act_t = attend(queries, kv[0], kv[1], lax.axis_index("seq") * token_count)
    act_top = jnp.max(jnp.abs(act_t)).astype(jnp.float32)
    share = token_count // n_tp
    pieces = []
    for k in range(n_tp):
        whose = lax.rem(tp_rank + k, n_tp)
        piece = lax.dynamic_slice_in_dim(act_t, whose * share, share, axis=1)
        pieces.append(piece if k == 0 else lax.ppermute(piece, "tp", shifts[k - 1]))
    act_peak = lax.pmax(act_top, ("seq", "tp")).reshape(1, 1)

    gain = norm_gain.astype(jnp.float32).reshape(1, d)
    new_residual, hidden, rstd, top = project(act_peak, pieces, w_own, w_peer, residual, gain)
    norm_peak = lax.pmax(top[0, 0], ("seq", "tp")).reshape(1, 1)
    next_input = final_quant(norm_peak, hidden, rstd, gain)
    return (new_residual, next_input)


def solution(mesh):
    in_specs = (
        P(("dp", "seq"), "tp"),
        P(("dp", "seq"), "tp"),
        P(("dp", "seq"), "tp"),
        P("tp", None),
        P(("dp", "seq", "tp"), None),
        P(),
    )
    out_specs = (P(("dp", "seq", "tp"), None), P(("dp", "seq", "tp"), None))
    return jax.shard_map(local, mesh=mesh, in_specs=in_specs, out_specs=out_specs, check_vma=False)
```

time: 347 us -> 191 us (0.55)
  other arithmetic: 150 us -> 12.5 us
  Pallas kernels: 0 us -> 77.8 us
  waiting for transfers between devices: 99.4 us -> 33.2 us
  matrix products: 26 us -> 8.99 us
  local copies, waits for them, and re-layouts: 18.3 us -> 4.71 us
  between operations: 18 us -> 14.1 us
  starting transfers between devices: 0.08 us -> 3.84 us
    convert_element_type x9 -> x0, other arithmetic: 108 us -> none  [the longest x3 96.1 us: fake_quant(): payload = soft_grid(blocks / spacing).astype(jnp.bfloat16)]
    reduce_scatter x1 -> x0, waiting for transfers between devices: 99.4 us -> none  [local(): lax.psum_scatter(lax.dot_general(act_q, weight_q, (((0,), (0,)), ((), ())...]
    pallas_call x0 -> x4, Pallas kernels: none -> 77.8 us  [the longest x1 28.8 us: final_quant(): pl.pallas_call(final_kernel, grid=(tokens // rows, d // width), in_specs=...]
    reduce_max x6 -> x1, other arithmetic: 29.7 us -> 5.13 us  [local(): weight_top = jnp.max(jnp.abs(out_weight)).astype(jnp.float32)]
    all_gather x1 -> x2, waiting for transfers between devices: 0.01 us -> 22.1 us  [the longest x1 22.1 us: local(): w_peer = lax.all_gather(from_peers, ('dp', 'seq'), axis=0)]
    dot_general x3 -> x2, matrix products: 26 us -> 8.99 us  [the longest x1 4.71 us: attend(): jnp.einsum('kgts,skd->kgtd', weights.astype(jnp.bfloat16), v, preferred_e...]
    ppermute x0 -> x2, waiting for transfers between devices: none -> 11 us  [the longest x1 11 us: local(): lax.ppermute(slab_q, 'tp', ring)]
    mul x1 -> x0, local copies, waits for them, and re-layouts: 9.02 us -> none  [local(): hidden_sum * lax.rsqrt(mean_square + 1e-05) * norm_gain.astype(jnp.float32)]
  transfers between devices with their start and end apart: 2 -> 4, of which waited for: 1 -> 2; matrix products, arithmetic and copies ran while one was open for 26% -> 12% of each run, Pallas kernels for 0% -> 14%
where the time goes in v1:
time: 191 us; the launch traced here: 190 us
  Pallas kernels  77.8 us (41%)
  blocking collectives  34.4 us (18%)
  waiting for transfers between devices  33.2 us (17%)
  between operations  14.1 us (7%)
  other arithmetic  12.5 us (7%)
  matrix products  8.99 us (5%)
  local copies, waits for them, and re-layouts  4.71 us (2%)
  starting transfers between devices  3.84 us (2%)
    pallas_call x1, Pallas kernels, final_quant(): pl.pallas_call(final_kernel, grid=(tokens // rows, d // width), in_specs=...  28.8 us
    pallas_call x2, Pallas kernels, quant_weight(): pl.pallas_call(functools.partial(quant_kernel, unroll=4), grid=(cols // w...  26.6 us
    pallas_call x1, Pallas kernels, project(): pl.pallas_call(functools.partial(project_kernel, n_tp=n_tp, n_feat=n_feat...  22.5 us
    all_gather x1, waiting for transfers between devices, local(): w_peer = lax.all_gather(from_peers, ('dp', 'seq'), axis=0)  22.1 us
    pmax x1, blocking collectives, local(): norm_peak = lax.pmax(top[0, 0], ('seq', 'tp')).reshape(1, 1)  14 us
    pmax x1, blocking collectives, local(): act_peak = lax.pmax(act_top, ('seq', 'tp')).reshape(1, 1)  13.9 us
    ppermute x1, waiting for transfers between devices, local(): lax.ppermute(slab_q, 'tp', ring)  11 us
    pmax x1, blocking collectives, local(): weight_peak = lax.pmax(weight_top, 'tp').reshape(1, 1)  6.48 us
  transfers between devices with their start and end apart: 4, of which 2 were waited for; matrix products, arithmetic and copies ran while one was open for 12% of the time, Pallas kernels for 14%

profile of v1, /device:TPU:0, one launch (start us, length us, event | category | flops | bytes accessed | tf_op | source)
XLA Modules:
  0.0 189.6 jit_solution(7010618477881542542)
XLA Ops:
  7.2 0.0 all-gather.4.cloned.1.call-start
  7.2 1.7 pad_maximum_fusion
  9.0 0.0 all-gather.6.cloned.1.call-start
  9.0 5.1 %abs_reduce_fusion = bf16[]{:T(256)} fusion(bf16[512,8192]{1,0:T(8,128)(2,1)} %w_ref.1), kind=kLoop, calls=%fused_computation.6 | loop fusion | flops 8388607 | bytes 8388610 | tf_op jit(solution)/shard_map/reduce_max | solution.py:229
  14.2 6.5 %pmax.22.peak_ref = f32[1,1]{1,0:T(1,128)} all-reduce(bf16[1,1]{1,0:T(2,128)(2,1)} %bitcast.21), channel_id=1, replica_groups=mesh['dp'=4,'seq'=4,'tp'=2] {'tp'}, use_global_device_ids=true, to_apply=%region_5.6 | all-reduce | flops 1 | bytes 6 | tf_op jit(solution)/shard_map/pmax | solution.py:230
  20.7 1.9 constant_dynamic-slice_fusion.w_ref
  22.5 3.6 %quant_weight.3 = bf16[512,512]{1,0:T(8,128)(2,1)} custom-call(f32[1,1]{1,0:T(1,128)} %pmax.22.peak_ref, bf16[512,512]{1,0:T(8,128)(2,1)} %constant_dynamic-slice_fusion.w_ref), custom_call_target="tpu_custom_call" | custom-call | flops 10485760 | bytes 1048576 | tf_op jit(solution)/shard_map/quant_weight/pallas_call | solution.py:60
  26.2 2.0 %collective-permute-start.1 = (bf16[512,512]{1,0:T(8,128)(2,1)}, bf16[512,512]{1,0:T(8,128)(2,1)S(1)}, u32[]{:S(2)}, u32[]{:S(2)}) collective-permute-start(bf16[512,512]{1,0:T(8,128)(2,1)} %quant_weight.3), channel_id=1, source_target_pairs={{0,1},{1,0},{2,3},{3,2},{4,5},{5,4},{6,7},{7,6},{8,9},{9,8},{10,11... | collective-permute-start | bytes 1572872 | tf_op jit(solution)/shard_map/ppermute | solution.py:235
  28.2 11.0 %collective-permute-done.1 = bf16[512,512]{1,0:T(8,128)(2,1)S(1)} collective-permute-done((bf16[512,512]{1,0:T(8,128)(2,1)}, bf16[512,512]{1,0:T(8,128)(2,1)S(1)}, u32[]{:S(2)}, u32[]{:S(2)}) %collective-permute-start.1) | collective-permute-done | bytes 524320 | tf_op jit(solution)/shard_map/ppermute | solution.py:235
  39.3 0.8 copy-done.2
  40.1 0.8 iota_compare_fusion
  41.0 4.3 %fusion = (f32[4,512]{1,0:T(4,128)S(1)}, f32[2048,512,4]{1,0,2:T(8,128)S(1)}) fusion(pred[512,2048]{0,1:T(8,128)(4,1)S(1)} %iota_compare_fusion, bf16[2,2048,128]{2,1,0:T(8,128)(2,1)} %all-gather.4.cloned.1.call-done, bf16[512,512]{1,0:T(8,128)(2,1)S(1)} %copy-done), kind=kOutput, calls=%fused_computation.2 | convolution fusion | flops 1086322688 | bytes 18882560 | tf_op jit(solution)/shard_map/tkgd,skd->kgts/dot_general | solution.py:204
  45.3 4.2 %fusion.1 = f32[4,512]{1,0:T(4,128)S(1)} fusion(f32[2048,512,4]{1,0,2:T(8,128)S(1)} %get-tuple-element.13, f32[4,512]{1,0:T(4,128)S(1)} %get-tuple-element.12, pred[512,2048]{0,1:T(8,128)(4,1)S(1)} %iota_compare_fusion), kind=kLoop, calls=%fused_computation.3 | loop fusion | flops 20969472 | bytes 17842176 | tf_op jit(solution)/shard_map/reduce_sum | solution.py:212
  49.5 4.7 %fusion.12 = (bf16[]{:T(256)}, bf16[4,512,128]{1,2,0:T(8,128)(2,1)S(1)}) fusion(f32[4,512]{1,0:T(4,128)S(1)} %fusion.1, bf16[2,2048,128]{2,1,0:T(8,128)(2,1)S(1)} %copy-done.5, f32[2048,512,4]{1,0,2:T(8,128)S(1)} %get-tuple-element.13, f32[4,512]{1,0:T(4,128)S(1)} %get-tuple-element.12, pred[512,2048]{0,1:T(8,128)(4,1)S(1)} %iota_compare_fusion), kind=kOutput, calls=%fused_computation.17 | convolution fusion | flops 1095761920 | bytes 18890754 | tf_op jit(solution)/shard_map/kgts,skd->kgtd/dot_general | solution.py:213
  54.2 0.7 constant_dynamic-slice_fusion.1
  54.9 1.7 collective-permute-start
  56.7 0.6 reshape.69
  57.3 22.9 %quant_weight.2.refs_3_ = bf16[512,8192]{1,0:T(8,128)(2,1)} custom-call(f32[1,1]{1,0:T(1,128)} %pmax.22.peak_ref, bf16[512,8192]{1,0:T(8,128)(2,1)} %w_ref.1), custom_call_target="tpu_custom_call" | custom-call | flops 167772160 | bytes 16777216 | tf_op jit(solution)/shard_map/quant_weight/pallas_call | solution.py:60
  80.2 13.9 %pmax.21.refs_0_ = f32[1,1]{1,0:T(1,128)} all-reduce(bf16[1,1]{1,0:T(2,128)(2,1)} %bitcast.20), channel_id=1, replica_groups=mesh['dp'=4,'seq'=4,'tp'=2] {'seq','tp'}, use_global_device_ids=true, to_apply=%region_3.4 | all-reduce | flops 1 | bytes 6 | tf_op jit(solution)/shard_map/pmax | solution.py:247
  94.1 22.1 %all-gather.6.cloned.1.call-done = bf16[8192,512]{1,0:T(8,128)(2,1)} async-done(((bf16[512,512]{1,0:T(8,128)(2,1)}), bf16[8192,512]{1,0:T(8,128)(2,1)}) %all-gather.6.cloned.1.call-update) | async-done | bytes 8388624 | tf_op jit(solution)/shard_map/all_gather | solution.py:236
  116.2 22.5 %project.1 = (bf16[256,8192]{1,0:T(8,128)(2,1)}, f32[256,8192]{1,0:T(8,128)}, f32[256,128]{1,0:T(8,128)}, f32[8,128]{1,0:T(8,128)}) custom-call(f32[1,1]{1,0:T(1,128)} %pmax.21.refs_0_, bf16[512,256]{1,0:T(8,128)(2,1)} %get-tuple-element.11.refs_1_, bf16[512,256]{1,0:T(8,128)(2,1)} %copy-done.3, bf16[512,8192]{1,0:T(8,128)(2,1)} %quant_weight.2.refs_3_, ...), custom_call_target="tpu_custom_call" | custom-call | flops 4294967296 | bytes 16777216 | tf_op jit(solution)/shard_map/project/pallas_call | solution.py:127
  138.7 1.3 slice.11
  140.0 14.0 %pmax.23.peak_ref = f32[1,1]{1,0:T(1,128)} all-reduce(f32[1,1]{1,0:T(1,128)} %slice.11), channel_id=1, replica_groups=mesh['dp'=4,'seq'=4,'tp'=2] {'seq','tp'}, use_global_device_ids=true, to_apply=%region_6.7 | all-reduce | flops 1 | bytes 8 | tf_op jit(solution)/shard_map/pmax | solution.py:251
  154.0 28.8 %final_quant.1 = bf16[256,8192]{1,0:T(8,128)(2,1)} custom-call(f32[1,1]{1,0:T(1,128)} %pmax.23.peak_ref, f32[256,8192]{1,0:T(8,128)} %get-tuple-element.8.hid_ref, f32[256,128]{1,0:T(8,128)} %get-tuple-element.9.rstd_ref, f32[1,8192]{1,0:T(1,128)} %bitcast.67), custom_call_target="tpu_custom_call" | custom-call | tf_op jit(solution)/shard_map/final_quant/pallas_call | solution.py:182
  (16 shorter events, 0.1 us)
Async XLA Ops:
  7.2 33.8 %copy-start = (bf16[512,512]{1,0:T(8,128)(2,1)S(1)}, bf16[512,512]{1,0:T(8,128)(2,1)}, u32[]{:S(2)}) copy-start(bf16[512,512]{1,0:T(8,128)(2,1)} %param.6) | copy-start | bytes 1572868
  7.2 33.8 %all-gather.4.cloned.1.call-start = ((), (), s32[]{:S(2)}) async-start(), calls=%async_computation | async-start | bytes 1310720 | tf_op jit(solution)/shard_map/all_gather | solution.py:227
  9.0 107.2 %all-gather.6.cloned.1.call-start = ((), (), s32[]{:S(2)}) async-start(), calls=%async_computation.1 | async-start | bytes 8912896 | tf_op jit(solution)/shard_map/all_gather | solution.py:236
  26.2 13.1 %collective-permute-start.1 = (bf16[512,512]{1,0:T(8,128)(2,1)}, bf16[512,512]{1,0:T(8,128)(2,1)S(1)}, u32[]{:S(2)}, u32[]{:S(2)}) collective-permute-start(bf16[512,512]{1,0:T(8,128)(2,1)} %quant_weight.3), channel_id=1, source_target_pairs={{0,1},{1,0},{2,3},{3,2},{4,5},{5,4},{6,7},{7,6},{8,9},{9,8},{10,11... | collective-permute-start | bytes 1572872 | tf_op jit(solution)/shard_map/ppermute | solution.py:235
  39.3 0.8 copy-start.2
  41.0 8.5 %copy-start.5 = (bf16[2,2048,128]{2,1,0:T(8,128)(2,1)S(1)}, bf16[2,2048,128]{2,1,0:T(8,128)(2,1)}, u32[]{:S(2)}) copy-start(bf16[2,2048,128]{2,1,0:T(8,128)(2,1)} %all-gather.4.cloned.1.call-done) | copy-start | bytes 3145732
  49.5 7.2 %copy-start.4 = (bf16[8192]{0:T(1024)(128)(2,1)S(1)}, bf16[8192]{0:T(1024)(128)(2,1)}, u32[]{:S(2)}) copy-start(bf16[8192]{0:T(1024)(128)(2,1)} %param.11) | copy-start | bytes 49156
  54.9 39.2 %collective-permute-start = (bf16[512,256]{1,0:T(8,128)(2,1)S(1)}, bf16[512,256]{1,0:T(8,128)(2,1)S(1)}, u32[]{:S(2)}, u32[]{:S(2)}) collective-permute-start(bf16[512,256]{1,0:T(8,128)(2,1)S(1)} %get-tuple-element.10), channel_id=1, source_target_pairs={{0,1},{1,0},{2,3},{3,2},{4,5},{5,4},{6,7},{7,6},{8,9},{9,8},{10,11... | collective-permute-start | bytes 786440 | tf_op jit(solution)/shard_map/ppermute | solution.py:246
  94.1 22.1 %copy-start.3 = (bf16[512,256]{1,0:T(8,128)(2,1)}, bf16[512,256]{1,0:T(8,128)(2,1)S(1)}, u32[]{:S(2)}) copy-start(bf16[512,256]{1,0:T(8,128)(2,1)S(1)} %collective-permute-done.refs_2_) | copy-start | bytes 786436
  116.2 66.6 %copy-start.1 = (bf16[512,512]{1,0:T(8,128)(2,1)S(1)}, bf16[512,512]{1,0:T(8,128)(2,1)}, u32[]{:S(2)}) copy-start(bf16[512,512]{1,0:T(8,128)(2,1)} %param.6) | copy-start | bytes 1572868
Sparse Core Ops, SparseCore 0:
  9.6 19.4 all-gather.3
  40.2 75.9 all-gather.5

commit v2 on v1

--- a/solution.py
+++ b/solution.py
@@ -55,14 +55,15 @@
     lax.fori_loop(0, rows // BLOCK, step, 0, unroll=unroll)
 
 
-def quant_weight(w, peak, width):
-    rows, cols = w.shape
+def quant_weight(w, peak, width, first, cols):
+    rows = w.shape[0]
+    skip = first // width
     return pl.pallas_call(
         functools.partial(quant_kernel, unroll=4),
         grid=(cols // width,),
         in_specs=[
             pl.BlockSpec(memory_space=pltpu.SMEM),
-            pl.BlockSpec((rows, width), lambda i: (0, i)),
+            pl.BlockSpec((rows, width), lambda i: (0, i + skip)),
         ],
         out_specs=pl.BlockSpec((rows, width), lambda i: (0, i)),
         out_shape=jax.ShapeDtypeStruct((rows, cols), jnp.bfloat16),
@@ -73,18 +74,18 @@
     )(peak, w)
 
 
-def project_kernel(*refs, n_tp, n_feat):
+def project_kernel(*refs, n_tp, n_feat, n_alias, features):
     peak_ref, act_refs = refs[0], refs[1 : 1 + n_tp]
-    own_ref, peer_ref, res_ref, gain_ref = refs[1 + n_tp : 5 + n_tp]
-    new_ref, hid_ref, rstd_ref, top_ref = refs[5 + n_tp : 9 + n_tp]
-    act_q, square_sum, row_top = refs[9 + n_tp :]
+    own_ref, peer_ref, res_ref, gain_ref, sq_in, top_in = refs[1 + n_tp : 7 + n_tp]
+    refs = refs[7 + n_tp + n_alias :]
+    new_ref, hid_ref, square_sum, row_top, rstd_ref, top_ref, act_q = refs
     step_id = pl.program_id(0)
 
     @pl.when(step_id == 0)
     def _():
         peak = peak_ref[0, 0]
-        square_sum[...] = jnp.zeros_like(square_sum)
-        row_top[...] = jnp.zeros_like(row_top)
+        square_sum[...] = sq_in[...]
+        row_top[...] = top_in[...]
         for k in range(n_tp):
             for lo in range(0, n_feat, 128):
                 x = act_refs[k][lo : lo + 128, :].astype(jnp.float32)
@@ -109,74 +110,85 @@
 
     @pl.when(step_id == pl.num_programs(0) - 1)
     def _():
-        width = hidden.shape[1] * pl.num_programs(0)
-        mean_square = jnp.sum(square_sum[...], axis=1, keepdims=True) / width
+        mean_square = jnp.sum(square_sum[...], axis=1, keepdims=True) / features
         rstd = lax.rsqrt(mean_square + 1e-05)
         rstd_ref[...] = jnp.broadcast_to(rstd, rstd_ref.shape)
         top_all = jnp.max(jnp.max(row_top[...], axis=1, keepdims=True) * rstd)
         top_ref[...] = jnp.full(top_ref.shape, top_all, jnp.float32)
 
 
-def project(peak, acts, w_own, w_peer, residual, gain):
+def project(peak, acts, w_own, w_peer, residual, gain, stats, width, skip, wide, made):
     n_tp = len(acts)
     n_feat, tokens = acts[0].shape
-    steps, _, _, width = w_peer.shape
     d = residual.shape[1]
-    column = pl.BlockSpec((tokens, width), lambda i: (0, i))
+    steps = w_own.shape[1] // width
+    column = pl.BlockSpec((tokens, width), lambda i: (0, i + skip))
     whole = pl.BlockSpec((tokens, 128), lambda i: (0, 0))
+    if wide:
+        peer_spec = pl.BlockSpec((1, n_tp - 1, n_feat, width), lambda i: (0, 0, 0, i))
+    else:
+        peer_spec = pl.BlockSpec((1, n_tp - 1, n_feat, width), lambda i: (i, 0, 0, 0))
+    stat = jax.ShapeDtypeStruct((tokens, 128), jnp.float32)
     return pl.pallas_call(
-        functools.partial(project_kernel, n_tp=n_tp, n_feat=n_feat),
+        functools.partial(project_kernel, n_tp=n_tp, n_feat=n_feat, n_alias=len(made), features=d),
         grid=(steps,),
         in_specs=[pl.BlockSpec(memory_space=pltpu.SMEM)]
         + [pl.BlockSpec((n_feat, tokens), lambda i: (0, 0))] * n_tp
         + [
             pl.BlockSpec((n_feat, width), lambda i: (0, i)),
-            pl.BlockSpec((1, n_tp - 1, n_feat, width), lambda i: (i, 0, 0, 0)),
+            peer_spec,
             column,
-            pl.BlockSpec((1, width), lambda i: (0, i)),
-        ],
-        out_specs=[column, column, whole, pl.BlockSpec((8, 128), lambda i: (0, 0))],
+            pl.BlockSpec((1, width), lambda i: (0, i + skip)),
+            whole,
+            whole,
+        ]
+        + [pl.BlockSpec(memory_space=pl.ANY)] * len(made),
+        out_specs=[column, column, whole, whole, whole, pl.BlockSpec((8, 128), lambda i: (0, 0))],
         out_shape=[
             jax.ShapeDtypeStruct((tokens, d), jnp.bfloat16),
             jax.ShapeDtypeStruct((tokens, d), jnp.float32),
-            jax.ShapeDtypeStruct((tokens, 128), jnp.float32),
+            stat,
+            stat,
+            stat,
             jax.ShapeDtypeStruct((8, 128), jnp.float32),
         ],
-        scratch_shapes=[
-            pltpu.VMEM((n_tp, tokens, n_feat), jnp.bfloat16),
-            pltpu.VMEM((tokens, 128), jnp.float32),
-            pltpu.VMEM((tokens, 128), jnp.float32),
-        ],
+        input_output_aliases={7 + n_tp + i: i for i in range(len(made))},
+        scratch_shapes=[pltpu.VMEM((n_tp, tokens, n_feat), jnp.bfloat16)],
         cost_estimate=pl.CostEstimate(
-            flops=2 * n_tp * n_feat * tokens * d, bytes_accessed=2 * n_tp * n_feat * d, transcendentals=0
+            flops=2 * n_tp * n_feat * tokens * steps * width,
+            bytes_accessed=2 * n_tp * n_feat * steps * width,
+            transcendentals=0,
         ),
         name="project",
-    )(peak, *acts, w_own, w_peer, residual, gain)
-
-
-def final_kernel(peak_ref, hid_ref, rstd_ref, gain_ref, out_ref):
+    )(peak, *acts, w_own, w_peer, residual, gain, *stats, *made)
+
+
+def final_kernel(peak_ref, hid_ref, rstd_ref, gain_ref, out_ref, narrow, wide):
     peak = peak_ref[0, 0]
-    rows = hid_ref.shape[0]
-    cols = hid_ref.shape[1]
+    rows, cols = hid_ref.shape
     src = lax.broadcasted_iota(jnp.int32, (128, 128), 0)
     dst = lax.broadcasted_iota(jnp.int32, (128, 128), 1)
     spread = jnp.where(src == (dst // BLOCK) * BLOCK + BLOCK - 1, 1.0, 0.0).astype(jnp.bfloat16)
     rstd = rstd_ref[...]
-    for lo in range(0, cols, 128):
-        x = hid_ref[:, lo : lo + 128] * rstd * gain_ref[:, lo : lo + 128]
+    tensor_scale = peak / (6.0 * 448.0)
+    pieces = cols // 128
+    for i in range(pieces):
+        x = hid_ref[:, i * 128 : i * 128 + 128] * rstd * gain_ref[:, i * 128 : i * 128 + 128]
         m = jnp.abs(x)
         for s in (1, 2, 4, 8):
             m = jnp.maximum(m, pltpu.roll(m, s, 1))
-        scale, tensor_scale = spacing_of(m, peak)
-        scale = jnp.dot(scale, spread, preferred_element_type=jnp.float32)
-        spacing = scale * tensor_scale
-        payload = soft_grid(x / spacing).astype(jnp.bfloat16).astype(jnp.float32)
-        out_ref[:, lo : lo + 128] = (payload * spacing).astype(jnp.bfloat16)
+        narrow[i * rows : (i + 1) * rows, :] = spacing_of(m, peak)[0]
+    wide[...] = jnp.dot(narrow[...], spread, preferred_element_type=jnp.float32)
+    for i in range(pieces):
+        x = hid_ref[:, i * 128 : i * 128 + 128] * rstd * gain_ref[:, i * 128 : i * 128 + 128]
+        spacing = wide[i * rows : (i + 1) * rows, :] * tensor_scale
+        payload = soft_grid(x * pl.reciprocal(spacing)).astype(jnp.bfloat16).astype(jnp.float32)
+        out_ref[:, i * 128 : i * 128 + 128] = (payload * spacing).astype(jnp.bfloat16)
 
 
 def final_quant(peak, hidden, rstd, gain):
     tokens, d = hidden.shape
-    width = 1024
+    width = 2048
     rows = min(64, tokens)
     column = pl.BlockSpec((rows, width), lambda i, j: (i, j))
     return pl.pallas_call(
@@ -190,6 +202,10 @@
         ],
         out_specs=column,
         out_shape=jax.ShapeDtypeStruct((tokens, d), jnp.bfloat16),
+        scratch_shapes=[
+            pltpu.VMEM((rows * width // 128, 128), jnp.bfloat16),
+            pltpu.VMEM((rows * width // 128, 128), jnp.float32),
+        ],
         name="final_quant",
     )(peak, hidden, rstd, gain)
 
@@ -229,12 +245,17 @@
     weight_top = jnp.max(jnp.abs(out_weight)).astype(jnp.float32)
     weight_peak = lax.pmax(weight_top, "tp").reshape(1, 1)
     slab_id = lax.axis_index("dp") * lax.axis_size("seq") + lax.axis_index("seq")
-    slab = lax.dynamic_slice_in_dim(out_weight, slab_id * width, width, axis=1)
-    slab_q = quant_weight(slab, weight_peak, width)
+    direct = 128
+    gather_w = width - direct
+    gathered = slabs * gather_w
+    slab = lax.dynamic_slice_in_dim(out_weight, slab_id * gather_w, gather_w, axis=1)
+    slab_q = quant_weight(slab, weight_peak, gather_w, 0, gather_w)
     shifts = [[(i, (i + k) % n_tp) for i in range(n_tp)] for k in range(1, n_tp)]
     from_peers = jnp.stack([lax.ppermute(slab_q, "tp", ring) for ring in shifts])
     w_peer = lax.all_gather(from_peers, ("dp", "seq"), axis=0)
-    w_own = quant_weight(out_weight, weight_peak, width)
+    near_own = quant_weight(out_weight, weight_peak, 512, gathered, d - gathered)
+    near_peer = jnp.stack([lax.ppermute(near_own, "tp", ring) for ring in shifts])[None]
+    w_own = quant_weight(out_weight, weight_peak, gather_w, 0, gathered)
 
     act_t = attend(queries, kv[0], kv[1], lax.axis_index("seq") * token_count)
     act_top = jnp.max(jnp.abs(act_t)).astype(jnp.float32)
@@ -247,7 +268,13 @@
     act_peak = lax.pmax(act_top, ("seq", "tp")).reshape(1, 1)
 
     gain = norm_gain.astype(jnp.float32).reshape(1, d)
-    new_residual, hidden, rstd, top = project(act_peak, pieces, w_own, w_peer, residual, gain)
+    stats = (jnp.zeros((share, 128), jnp.float32),) * 2
+    near = project(
+        act_peak, pieces, near_own, near_peer, residual, gain, stats, 512, gathered // 512, True, ()
+    )
+    new_residual, hidden, _, _, rstd, top = project(
+        act_peak, pieces, w_own, w_peer, residual, gain, near[2:4], gather_w, 0, False, near[:2]
+    )
     norm_peak = lax.pmax(top[0, 0], ("seq", "tp")).reshape(1, 1)
     next_input = final_quant(norm_peak, hidden, rstd, gain)
     return (new_residual, next_input)

time: 191 us -> 178 us (0.932)
  waiting for transfers between devices: 33.2 us -> 8.28 us
  blocking collectives: 34.4 us -> 42.4 us
  Pallas kernels: 77.8 us -> 80.2 us
    all_gather x1, waiting for transfers between devices: 22.1 us -> 0.02 us  [local(): w_peer = lax.all_gather(from_peers, ('dp', 'seq'), axis=0)]
    pmax x1, blocking collectives: 13.9 us -> 23.2 us  [local(): act_peak = lax.pmax(act_top, ('seq', 'tp')).reshape(1, 1)]
    pallas_call x1, Pallas kernels: 28.8 us -> 20.9 us  [final_quant(): pl.pallas_call(final_kernel, grid=(tokens // rows, d // width), in_specs=...]
    pallas_call x1 -> x2, Pallas kernels: 22.5 us -> 28 us  [project(): pl.pallas_call(functools.partial(project_kernel, n_tp=n_tp, n_feat=n_feat...]
    pallas_call x2 -> x3, Pallas kernels: 26.6 us -> 31.3 us  [quant_weight(): pl.pallas_call(functools.partial(quant_kernel, unroll=4), grid=(cols // w...]
    ppermute x1, waiting for transfers between devices: 11 us -> 8.2 us  [local(): lax.ppermute(slab_q, 'tp', ring)]
  transfers between devices with their start and end apart: 4 -> 5, of which waited for: 2 -> 1; matrix products, arithmetic and copies ran while one was open for 12% -> 13% of each run, Pallas kernels for 14% -> 23%
where the time goes in v2:
time: 178 us; the launch traced here: 176 us
  Pallas kernels  80.2 us (45%)
  blocking collectives  42.4 us (24%)
  between operations  14.1 us (8%)
  other arithmetic  12.5 us (7%)
  matrix products  8.99 us (5%)
  waiting for transfers between devices  8.28 us (5%)
  local copies, waits for them, and re-layouts  5.26 us (3%)
  starting transfers between devices  4.18 us (2%)
    pallas_call x3, Pallas kernels, quant_weight(): pl.pallas_call(functools.partial(quant_kernel, unroll=4), grid=(cols // w...  31.3 us
    pallas_call x2, Pallas kernels, project(): pl.pallas_call(functools.partial(project_kernel, n_tp=n_tp, n_feat=n_feat...  28 us
    pmax x1, blocking collectives, local(): act_peak = lax.pmax(act_top, ('seq', 'tp')).reshape(1, 1)  23.2 us
    pallas_call x1, Pallas kernels, final_quant(): pl.pallas_call(final_kernel, grid=(tokens // rows, d // width), in_specs=...  20.9 us
    pmax x1, blocking collectives, local(): norm_peak = lax.pmax(top[0, 0], ('seq', 'tp')).reshape(1, 1)  12.6 us
    ppermute x1, waiting for transfers between devices, local(): lax.ppermute(slab_q, 'tp', ring)  8.2 us
    pmax x1, blocking collectives, local(): weight_peak = lax.pmax(weight_top, 'tp').reshape(1, 1)  6.54 us
    reduce_max x1, other arithmetic, local(): weight_top = jnp.max(jnp.abs(out_weight)).astype(jnp.float32)  5.13 us
  transfers between devices with their start and end apart: 5, of which 1 were waited for; matrix products, arithmetic and copies ran while one was open for 13% of the time, Pallas kernels for 23%

profile of v2, /device:TPU:0, one launch (start us, length us, event | category | flops | bytes accessed | tf_op | source)
XLA Modules:
  0.0 175.9 jit_solution(2849412599000884221)
XLA Ops:
  7.2 1.7 pad_maximum_fusion
  9.1 5.1 %abs_reduce_fusion = bf16[]{:T(256)} fusion(bf16[512,8192]{1,0:T(8,128)(2,1)} %w_ref.3), kind=kLoop, calls=%fused_computation.6 | loop fusion | flops 8388607 | bytes 8388610 | tf_op jit(solution)/shard_map/reduce_max | solution.py:245
  14.2 6.5 %pmax.22.peak_ref = f32[1,1]{1,0:T(1,128)} all-reduce(bf16[1,1]{1,0:T(2,128)(2,1)} %bitcast.22), channel_id=1, replica_groups=mesh['dp'=4,'seq'=4,'tp'=2] {'tp'}, use_global_device_ids=true, to_apply=%region_5.6 | all-reduce | flops 1 | bytes 6 | tf_op jit(solution)/shard_map/pmax | solution.py:246
  20.7 1.8 %constant_dynamic-slice_fusion.w_ref = bf16[512,384]{1,0:T(8,128)(2,1)} fusion(bf16[512,8192]{1,0:T(8,128)(2,1)} %w_ref.3, s32[]{:T(128)S(6)} %select_n.20), kind=kLoop, calls=%fused_computation.20 | loop fusion | bytes 786436 | tf_op jit(solution)/shard_map/dynamic_slice | solution.py:251
  22.5 3.4 %quant_weight.4 = bf16[512,384]{1,0:T(8,128)(2,1)} custom-call(f32[1,1]{1,0:T(1,128)} %pmax.22.peak_ref, bf16[512,384]{1,0:T(8,128)(2,1)} %constant_dynamic-slice_fusion.w_ref), custom_call_target="tpu_custom_call" | custom-call | flops 7864320 | bytes 786432 | tf_op jit(solution)/shard_map/quant_weight/pallas_call | solution.py:61
  25.9 2.0 %collective-permute-start.1 = (bf16[512,384]{1,0:T(8,128)(2,1)}, bf16[512,384]{1,0:T(8,128)(2,1)S(1)}, u32[]{:S(2)}, u32[]{:S(2)}) collective-permute-start(bf16[512,384]{1,0:T(8,128)(2,1)} %quant_weight.4), channel_id=1, source_target_pairs={{0,1},{1,0},{2,3},{3,2},{4,5},{5,4},{6,7},{7,6},{8,9},{9,8},{10,11... | collective-permute-start | bytes 1179656 | tf_op jit(solution)/shard_map/ppermute | solution.py:254
  28.0 8.2 %collective-permute-done.1 = bf16[512,384]{1,0:T(8,128)(2,1)S(1)} collective-permute-done((bf16[512,384]{1,0:T(8,128)(2,1)}, bf16[512,384]{1,0:T(8,128)(2,1)S(1)}, u32[]{:S(2)}, u32[]{:S(2)}) %collective-permute-start.1) | collective-permute-done | bytes 393248 | tf_op jit(solution)/shard_map/ppermute | solution.py:254
  36.2 0.8 copy-done.3
  37.0 7.6 %quant_weight.5.refs_3_ = bf16[512,2048]{1,0:T(8,128)(2,1)} custom-call(f32[1,1]{1,0:T(1,128)} %pmax.22.peak_ref, bf16[512,8192]{1,0:T(8,128)(2,1)} %w_ref.3), custom_call_target="tpu_custom_call" | custom-call | flops 41943040 | bytes 4194304 | tf_op jit(solution)/shard_map/quant_weight/pallas_call | solution.py:61
  44.5 1.7 collective-permute-start.2
  46.3 0.8 iota_compare_fusion
  47.1 4.3 %fusion = (f32[4,512]{1,0:T(4,128)S(1)}, f32[2048,512,4]{1,0,2:T(8,128)S(1)}) fusion(pred[512,2048]{0,1:T(8,128)(4,1)S(1)} %iota_compare_fusion, bf16[2,2048,128]{2,1,0:T(8,128)(2,1)} %all-gather.4.cloned.1.call-done, bf16[512,512]{1,0:T(8,128)(2,1)S(1)} %copy-done), kind=kOutput, calls=%fused_computation.2 | convolution fusion | flops 1086322688 | bytes 18882560 | tf_op jit(solution)/shard_map/tkgd,skd->kgts/dot_general | solution.py:220
  51.4 4.2 %fusion.1 = f32[4,512]{1,0:T(4,128)S(1)} fusion(f32[2048,512,4]{1,0,2:T(8,128)S(1)} %get-tuple-element.21, f32[4,512]{1,0:T(4,128)S(1)} %get-tuple-element.20, pred[512,2048]{0,1:T(8,128)(4,1)S(1)} %iota_compare_fusion), kind=kLoop, calls=%fused_computation.3 | loop fusion | flops 20969472 | bytes 17842176 | tf_op jit(solution)/shard_map/reduce_sum | solution.py:228
  55.6 4.7 %fusion.12 = (bf16[]{:T(256)}, bf16[4,512,128]{1,2,0:T(8,128)(2,1)S(1)}) fusion(f32[4,512]{1,0:T(4,128)S(1)} %fusion.1, bf16[2,2048,128]{2,1,0:T(8,128)(2,1)S(1)} %copy-done.5, f32[2048,512,4]{1,0,2:T(8,128)S(1)} %get-tuple-element.21, f32[4,512]{1,0:T(4,128)S(1)} %get-tuple-element.20, pred[512,2048]{0,1:T(8,128)(4,1)S(1)} %iota_compare_fusion), kind=kOutput, calls=%fused_computation.17 | convolution fusion | flops 1095761920 | bytes 18890754 | tf_op jit(solution)/shard_map/kgts,skd->kgtd/dot_general | solution.py:229
  60.3 0.7 constant_dynamic-slice_fusion.1
  61.4 0.6 reshape.69
  62.0 20.3 %quant_weight.3.refs_3_ = bf16[512,6144]{1,0:T(8,128)(2,1)} custom-call(f32[1,1]{1,0:T(1,128)} %pmax.22.peak_ref, bf16[512,8192]{1,0:T(8,128)(2,1)} %w_ref.3), custom_call_target="tpu_custom_call" | custom-call | flops 125829120 | bytes 12582912 | tf_op jit(solution)/shard_map/quant_weight/pallas_call | solution.py:61
  82.3 23.2 %pmax.21.refs_0_ = f32[1,1]{1,0:T(1,128)} all-reduce(bf16[1,1]{1,0:T(2,128)(2,1)} %bitcast.21), channel_id=1, replica_groups=mesh['dp'=4,'seq'=4,'tp'=2] {'seq','tp'}, use_global_device_ids=true, to_apply=%region_3.4 | all-reduce | flops 1 | bytes 6 | tf_op jit(solution)/shard_map/pmax | solution.py:268
  105.5 0.7 broadcast_in_dim.20.refs_7_.refs_8_
  106.3 8.5 %project.2 = (bf16[256,8192]{1,0:T(8,128)(2,1)}, f32[256,8192]{1,0:T(8,128)}, f32[256,128]{1,0:T(8,128)}, f32[256,128]{1,0:T(8,128)}, f32[256,128]{1,0:T(8,128)}, /*index=5*/f32[8,128]{1,0:T(8,128)}) custom-call(f32[1,1]{1,0:T(1,128)} %pmax.21.refs_0_, bf16[512,256]{1,0:T(8,128)(2,1)} %get-tuple-element.19.refs_1_, bf16[512,256]{1,0:T(8,128)(2,1)} %copy-done.2, ...), custom_call_target="tpu_custom_call" | custom-call | flops 1073741824 | bytes 4194304 | tf_op jit(solution)/shard_map/project/pallas_call | solution.py:132
  114.8 19.5 %project.3 = (bf16[256,8192]{1,0:T(8,128)(2,1)}, f32[256,8192]{1,0:T(8,128)}, f32[256,128]{1,0:T(8,128)}, f32[256,128]{1,0:T(8,128)}, f32[256,128]{1,0:T(8,128)}, /*index=5*/f32[8,128]{1,0:T(8,128)}) custom-call(f32[1,1]{1,0:T(1,128)} %pmax.21.refs_0_, bf16[512,256]{1,0:T(8,128)(2,1)} %get-tuple-element.19.refs_1_, ...), custom_call_target="tpu_custom_call", output_to_operand_aliasing={{0}: (9, {}), {1}: (10, {})} | custom-call | flops 3221225472 | bytes 12582912 | tf_op jit(solution)/shard_map/project/pallas_call | solution.py:132
  134.3 1.2 slice.11
  135.5 12.6 %pmax.23.peak_ref = f32[1,1]{1,0:T(1,128)} all-reduce(f32[1,1]{1,0:T(1,128)} %slice.11), channel_id=1, replica_groups=mesh['dp'=4,'seq'=4,'tp'=2] {'seq','tp'}, use_global_device_ids=true, to_apply=%region_6.7 | all-reduce | flops 1 | bytes 8 | tf_op jit(solution)/shard_map/pmax | solution.py:278
  148.1 20.9 %final_quant.1 = bf16[256,8192]{1,0:T(8,128)(2,1)} custom-call(f32[1,1]{1,0:T(1,128)} %pmax.23.peak_ref, f32[256,8192]{1,0:T(8,128)} %get-tuple-element.16.hid_ref, f32[256,128]{1,0:T(8,128)} %get-tuple-element.17.rstd_ref, f32[1,8192]{1,0:T(1,128)} %bitcast.68), custom_call_target="tpu_custom_call" | custom-call | tf_op jit(solution)/shard_map/final_quant/pallas_call | solution.py:194
  (21 shorter events, 0.6 us)
Async XLA Ops:
  7.2 40.0 %copy-start = (bf16[512,512]{1,0:T(8,128)(2,1)S(1)}, bf16[512,512]{1,0:T(8,128)(2,1)}, u32[]{:S(2)}) copy-start(bf16[512,512]{1,0:T(8,128)(2,1)} %param.6) | copy-start | bytes 1572868
  7.2 39.9 %all-gather.4.cloned.1.call-start = ((), (), s32[]{:S(2)}) async-start(), calls=%async_computation | async-start | bytes 1310720 | tf_op jit(solution)/shard_map/all_gather | solution.py:243
  9.0 105.8 %all-gather.6.cloned.1.call-start = ((), (), s32[]{:S(2)}) async-start(), calls=%async_computation.1 | async-start | bytes 6684672 | tf_op jit(solution)/shard_map/all_gather | solution.py:255
  25.9 10.2 %collective-permute-start.1 = (bf16[512,384]{1,0:T(8,128)(2,1)}, bf16[512,384]{1,0:T(8,128)(2,1)S(1)}, u32[]{:S(2)}, u32[]{:S(2)}) collective-permute-start(bf16[512,384]{1,0:T(8,128)(2,1)} %quant_weight.4), channel_id=1, source_target_pairs={{0,1},{1,0},{2,3},{3,2},{4,5},{5,4},{6,7},{7,6},{8,9},{9,8},{10,11... | collective-permute-start | bytes 1179656 | tf_op jit(solution)/shard_map/ppermute | solution.py:254
  36.2 0.8 copy-start.3
  44.5 61.0 %collective-permute-start.2 = (bf16[512,2048]{1,0:T(8,128)(2,1)}, bf16[512,2048]{1,0:T(8,128)(2,1)}, u32[]{:S(2)}, u32[]{:S(2)}) collective-permute-start(bf16[512,2048]{1,0:T(8,128)(2,1)} %quant_weight.5.refs_3_), channel_id=1, source_target_pairs={{0,1},{1,0},{2,3},{3,2},{4,5},{5,4},{6,7},{7,6},{8,9},{9,8},{10,11... | collective-permute-start | bytes 6291464 | tf_op jit(solution)/shard_map/ppermute | solution.py:257
  47.1 8.5 %copy-start.5 = (bf16[2,2048,128]{2,1,0:T(8,128)(2,1)S(1)}, bf16[2,2048,128]{2,1,0:T(8,128)(2,1)}, u32[]{:S(2)}) copy-start(bf16[2,2048,128]{2,1,0:T(8,128)(2,1)} %all-gather.4.cloned.1.call-done) | copy-start | bytes 3145732
  55.6 5.8 %copy-start.4 = (bf16[8192]{0:T(1024)(128)(2,1)S(1)}, bf16[8192]{0:T(1024)(128)(2,1)}, u32[]{:S(2)}) copy-start(bf16[8192]{0:T(1024)(128)(2,1)} %param.11) | copy-start | bytes 49156
  61.1 44.4 %collective-permute-start = (bf16[512,256]{1,0:T(8,128)(2,1)S(1)}, bf16[512,256]{1,0:T(8,128)(2,1)S(1)}, u32[]{:S(2)}, u32[]{:S(2)}) collective-permute-start(bf16[512,256]{1,0:T(8,128)(2,1)S(1)} %get-tuple-element.18), channel_id=1, source_target_pairs={{0,1},{1,0},{2,3},{3,2},{4,5},{5,4},{6,7},{7,6},{8,9},{9,8},{10,11... | collective-permute-start | bytes 786440 | tf_op jit(solution)/shard_map/ppermute | solution.py:267
  105.5 0.8 copy-start.2
  114.8 54.3 %copy-start.1 = (bf16[512,512]{1,0:T(8,128)(2,1)S(1)}, bf16[512,512]{1,0:T(8,128)(2,1)}, u32[]{:S(2)}) copy-start(bf16[512,512]{1,0:T(8,128)(2,1)} %param.6) | copy-start | bytes 1572868
Sparse Core Ops, SparseCore 0:
  9.6 19.4 all-gather.3
  37.1 62.9 all-gather.5

commit v3 on v2

--- a/solution.py
+++ b/solution.py
@@ -233,6 +233,10 @@
     return attended.transpose(0, 1, 3, 2).reshape(-1, token_count)
 
 
+def peak_over(value, axes):
+    return jnp.max(lax.all_gather(value.reshape(1, 1), axes)).reshape(1, 1)
+
+
 def local(queries, keys, values, out_weight, residual, norm_gain):
     token_count = queries.shape[0]
     n_tp = lax.axis_size("tp")
@@ -243,7 +247,7 @@
     kv = lax.all_gather(jnp.stack((keys, values)), "seq", axis=1, tiled=True)
 
     weight_top = jnp.max(jnp.abs(out_weight)).astype(jnp.float32)
-    weight_peak = lax.pmax(weight_top, "tp").reshape(1, 1)
+    weight_peak = peak_over(weight_top, "tp")
     slab_id = lax.axis_index("dp") * lax.axis_size("seq") + lax.axis_index("seq")
     direct = 128
     gather_w = width - direct
@@ -265,7 +269,7 @@
         whose = lax.rem(tp_rank + k, n_tp)
         piece = lax.dynamic_slice_in_dim(act_t, whose * share, share, axis=1)
         pieces.append(piece if k == 0 else lax.ppermute(piece, "tp", shifts[k - 1]))
-    act_peak = lax.pmax(act_top, ("seq", "tp")).reshape(1, 1)
+    act_peak = peak_over(act_top, ("seq", "tp"))
 
     gain = norm_gain.astype(jnp.float32).reshape(1, d)
     stats = (jnp.zeros((share, 128), jnp.float32),) * 2
@@ -275,7 +279,7 @@
     new_residual, hidden, _, _, rstd, top = project(
         act_peak, pieces, w_own, w_peer, residual, gain, near[2:4], gather_w, 0, False, near[:2]
     )
-    norm_peak = lax.pmax(top[0, 0], ("seq", "tp")).reshape(1, 1)
+    norm_peak = peak_over(top[0, 0], ("seq", "tp"))
     next_input = final_quant(norm_peak, hidden, rstd, gain)
     return (new_residual, next_input)
 

time: 178 us -> 182 us (1.022)
  other arithmetic: 12.5 us -> 17.1 us
  blocking collectives: 42.4 us -> 39 us
  local copies, waits for them, and re-layouts: 5.26 us -> 8.44 us
    pmax x3 -> x0, blocking collectives: 42.4 us -> none  [the longest x1 23.2 us: local(): act_peak = lax.pmax(act_top, ('seq', 'tp')).reshape(1, 1)]
    unnamed x0 -> x3, blocking collectives: none -> 39 us
    unnamed x12 -> x20, local copies, waits for them, and re-layouts: 0.86 us -> 4.03 us
    unnamed x0 -> x2, other arithmetic: none -> 2.76 us
    reduce_max x0 -> x3, other arithmetic: none -> 1.86 us  [peak_over(): return jnp.max(lax.all_gather(value.reshape(1, 1), axes)).reshape(1, 1)]
  transfers between devices with their start and end apart: 5 -> 5, of which waited for: 1 -> 1; matrix products, arithmetic and copies ran while one was open for 13% -> 16% of each run, Pallas kernels for 23% -> 22%
where the time goes in v3:
time: 182 us; the launch traced here: 180 us
  Pallas kernels  80.1 us (44%)
  blocking collectives  39 us (21%)
  other arithmetic  17.1 us (9%)
  between operations  14.2 us (8%)
  matrix products  9.05 us (5%)
  local copies, waits for them, and re-layouts  8.44 us (5%)
  waiting for transfers between devices  8.26 us (5%)
  starting transfers between devices  4.1 us (2%)
    unnamed x3, blocking collectives  39 us
    pallas_call x3, Pallas kernels, quant_weight(): pl.pallas_call(functools.partial(quant_kernel, unroll=4), grid=(cols // w...  31.3 us
    pallas_call x2, Pallas kernels, project(): pl.pallas_call(functools.partial(project_kernel, n_tp=n_tp, n_feat=n_feat...  27.8 us
    pallas_call x1, Pallas kernels, final_quant(): pl.pallas_call(final_kernel, grid=(tokens // rows, d // width), in_specs=...  20.9 us
    ppermute x1, waiting for transfers between devices, local(): lax.ppermute(slab_q, 'tp', ring)  8.18 us
    reduce_max x1, other arithmetic, local(): weight_top = jnp.max(jnp.abs(out_weight)).astype(jnp.float32)  5.13 us
    dot_general x1, matrix products, attend(): jnp.einsum('kgts,skd->kgtd', weights.astype(jnp.bfloat16), v, preferred_e...  4.71 us
    dot_general x1, matrix products, attend(): jnp.einsum('tkgd,skd->kgts', q, k, preferred_element_type=jnp.float32)  4.34 us
  transfers between devices with their start and end apart: 5, of which 1 were waited for; matrix products, arithmetic and copies ran while one was open for 16% of the time, Pallas kernels for 22%

profile of v3, /device:TPU:0, one launch (start us, length us, event | category | flops | bytes accessed | tf_op | source)
XLA Modules:
  0.0 180.2 jit_solution(15817859898578933934)
XLA Ops:
  7.2 1.7 pad_maximum_fusion
  9.1 1.2 dynamic-slice.1
  10.3 5.1 %abs_reduce_fusion = bf16[]{:T(256)} fusion(bf16[512,8192]{1,0:T(8,128)(2,1)} %w_ref.3), kind=kLoop, calls=%fused_computation.6 | loop fusion | flops 8388607 | bytes 8388610 | tf_op jit(solution)/shard_map/reduce_max | solution.py:249
  15.4 1.4 convert_dynamic-update-slice_fusion
  16.8 5.8 %all-reduce.1 = f32[2]{0:T(128)S(1)} all-reduce(f32[2]{0:T(128)S(1)} %convert_dynamic-update-slice_fusion), channel_id=1, replica_groups=mesh['dp'=4,'seq'=4,'tp'=2] {'tp'}, use_global_device_ids=true, to_apply=%add.1 | all-reduce | flops 2 | bytes 16
  23.3 1.8 constant_dynamic-slice_fusion.w_ref
  25.1 3.4 %quant_weight.4 = bf16[512,384]{1,0:T(8,128)(2,1)} custom-call(f32[1,1]{1,0:T(1,128)} %bitcast.19.peak_ref, bf16[512,384]{1,0:T(8,128)(2,1)} %constant_dynamic-slice_fusion.w_ref), custom_call_target="tpu_custom_call" | custom-call | flops 7864320 | bytes 786432 | tf_op jit(solution)/shard_map/quant_weight/pallas_call | solution.py:61
  28.5 2.0 %collective-permute-start.1 = (bf16[512,384]{1,0:T(8,128)(2,1)}, bf16[512,384]{1,0:T(8,128)(2,1)S(1)}, u32[]{:S(2)}, u32[]{:S(2)}) collective-permute-start(bf16[512,384]{1,0:T(8,128)(2,1)} %quant_weight.4), channel_id=1, source_target_pairs={{0,1},{1,0},{2,3},{3,2},{4,5},{5,4},{6,7},{7,6},{8,9},{9,8},{10,11... | collective-permute-start | bytes 1179656 | tf_op jit(solution)/shard_map/ppermute | solution.py:258
  30.6 8.2 %collective-permute-done.1 = bf16[512,384]{1,0:T(8,128)(2,1)S(1)} collective-permute-done((bf16[512,384]{1,0:T(8,128)(2,1)}, bf16[512,384]{1,0:T(8,128)(2,1)S(1)}, u32[]{:S(2)}, u32[]{:S(2)}) %collective-permute-start.1) | collective-permute-done | bytes 393248 | tf_op jit(solution)/shard_map/ppermute | solution.py:258
  39.5 7.6 %quant_weight.5.refs_3_ = bf16[512,2048]{1,0:T(8,128)(2,1)} custom-call(f32[1,1]{1,0:T(1,128)} %bitcast.19.peak_ref, bf16[512,8192]{1,0:T(8,128)(2,1)} %w_ref.3), custom_call_target="tpu_custom_call" | custom-call | flops 41943040 | bytes 4194304 | tf_op jit(solution)/shard_map/quant_weight/pallas_call | solution.py:61
  47.1 1.7 collective-permute-start.2
  48.8 0.8 iota_compare_fusion
  49.7 4.3 %fusion = (f32[4,512]{1,0:T(4,128)S(1)}, f32[2048,512,4]{1,0,2:T(8,128)S(1)}) fusion(pred[512,2048]{0,1:T(8,128)(4,1)S(1)} %iota_compare_fusion, bf16[2,2048,128]{2,1,0:T(8,128)(2,1)} %all-gather.5.cloned.1.call-done, bf16[512,512]{1,0:T(8,128)(2,1)S(1)} %copy-done), kind=kOutput, calls=%fused_computation.2 | convolution fusion | flops 1086322688 | bytes 18882560 | tf_op jit(solution)/shard_map/tkgd,skd->kgts/dot_general | solution.py:220
  54.1 4.2 %fusion.1 = f32[4,512]{1,0:T(4,128)S(1)} fusion(f32[2048,512,4]{1,0,2:T(8,128)S(1)} %get-tuple-element.21, f32[4,512]{1,0:T(4,128)S(1)} %get-tuple-element.20, pred[512,2048]{0,1:T(8,128)(4,1)S(1)} %iota_compare_fusion), kind=kLoop, calls=%fused_computation.3 | loop fusion | flops 20969472 | bytes 17842176 | tf_op jit(solution)/shard_map/reduce_sum | solution.py:228
  58.3 4.7 %fusion.12 = (bf16[]{:T(256)}, bf16[4,512,128]{1,2,0:T(8,128)(2,1)S(1)}) fusion(f32[4,512]{1,0:T(4,128)S(1)} %fusion.1, bf16[2,2048,128]{2,1,0:T(8,128)(2,1)S(1)} %copy-done.5, f32[2048,512,4]{1,0,2:T(8,128)S(1)} %get-tuple-element.21, f32[4,512]{1,0:T(4,128)S(1)} %get-tuple-element.20, pred[512,2048]{0,1:T(8,128)(4,1)S(1)} %iota_compare_fusion), kind=kOutput, calls=%fused_computation.17 | convolution fusion | flops 1095761920 | bytes 18890754 | tf_op jit(solution)/shard_map/kgts,skd->kgtd/dot_general | solution.py:229
  64.6 20.3 %quant_weight.3.refs_3_ = bf16[512,6144]{1,0:T(8,128)(2,1)} custom-call(f32[1,1]{1,0:T(1,128)} %bitcast.19.peak_ref, bf16[512,8192]{1,0:T(8,128)(2,1)} %w_ref.3), custom_call_target="tpu_custom_call" | custom-call | flops 125829120 | bytes 12582912 | tf_op jit(solution)/shard_map/quant_weight/pallas_call | solution.py:61
  84.9 1.4 convert_dynamic-update-slice_fusion.1
  86.9 20.6 %all-reduce = f32[8]{0:T(128)S(1)} all-reduce(f32[8]{0:T(128)S(1)} %convert_dynamic-update-slice_fusion.1), channel_id=1, replica_groups=mesh['dp'=4,'seq'=4,'tp'=2] {'seq','tp'}, use_global_device_ids=true, to_apply=%add | all-reduce | flops 8 | bytes 64
  108.9 8.4 %project.2 = (bf16[256,8192]{1,0:T(8,128)(2,1)}, f32[256,8192]{1,0:T(8,128)}, f32[256,128]{1,0:T(8,128)}, f32[256,128]{1,0:T(8,128)}, f32[256,128]{1,0:T(8,128)}, /*index=5*/f32[8,128]{1,0:T(8,128)}) custom-call(f32[1,1]{1,0:T(1,128)} %bitcast.13.refs_0_, bf16[512,256]{1,0:T(8,128)(2,1)} %get-tuple-element.19.refs_1_, bf16[512,256]{1,0:T(8,128)(2,1)} %copy-done.2, ...), custom_call_target="tpu_custom_call" | custom-call | flops 1073741824 | bytes 4194304 | tf_op jit(solution)/shard_map/project/pallas_call | solution.py:132
  117.4 19.4 %project.3 = (bf16[256,8192]{1,0:T(8,128)(2,1)}, f32[256,8192]{1,0:T(8,128)}, f32[256,128]{1,0:T(8,128)}, f32[256,128]{1,0:T(8,128)}, f32[256,128]{1,0:T(8,128)}, /*index=5*/f32[8,128]{1,0:T(8,128)}) custom-call(f32[1,1]{1,0:T(1,128)} %bitcast.13.refs_0_, bf16[512,256]{1,0:T(8,128)(2,1)} %get-tuple-element.19.refs_1_, ...), custom_call_target="tpu_custom_call", output_to_operand_aliasing={{0}: (9, {}), {1}: (10, {})} | custom-call | flops 3221225472 | bytes 12582912 | tf_op jit(solution)/shard_map/project/pallas_call | solution.py:132
  136.8 1.2 slice.11
  138.0 1.3 bitcast_dynamic-update-slice_fusion
  139.3 12.5 %all-reduce.2 = f32[8]{0:T(128)S(1)} all-reduce(f32[8]{0:T(128)S(1)} %bitcast_dynamic-update-slice_fusion), channel_id=3, replica_groups=mesh['dp'=4,'seq'=4,'tp'=2] {'seq','tp'}, use_global_device_ids=true, to_apply=%add.2 | all-reduce | flops 8 | bytes 64
  152.4 20.9 %final_quant.1 = bf16[256,8192]{1,0:T(8,128)(2,1)} custom-call(f32[1,1]{1,0:T(1,128)} %bitcast.24.peak_ref, f32[256,8192]{1,0:T(8,128)} %get-tuple-element.16.hid_ref, f32[256,128]{1,0:T(8,128)} %get-tuple-element.17.rstd_ref, f32[1,8192]{1,0:T(1,128)} %bitcast.75), custom_call_target="tpu_custom_call" | custom-call | tf_op jit(solution)/shard_map/final_quant/pallas_call | solution.py:194
  (34 shorter events, 5.8 us)
Async XLA Ops:
  7.2 42.5 %copy-start = (bf16[512,512]{1,0:T(8,128)(2,1)S(1)}, bf16[512,512]{1,0:T(8,128)(2,1)}, u32[]{:S(2)}) copy-start(bf16[512,512]{1,0:T(8,128)(2,1)} %param.6) | copy-start | bytes 1572868
  7.2 42.5 %all-gather.5.cloned.1.call-start = ((), (), s32[]{:S(2)}) async-start(), calls=%async_computation | async-start | bytes 1310720 | tf_op jit(solution)/shard_map/all_gather | solution.py:247
  9.0 108.4 %all-gather.7.cloned.1.call-start = ((), (), s32[]{:S(2)}) async-start(), calls=%async_computation.1 | async-start | bytes 6684672 | tf_op jit(solution)/shard_map/all_gather | solution.py:259
  28.5 10.2 %collective-permute-start.1 = (bf16[512,384]{1,0:T(8,128)(2,1)}, bf16[512,384]{1,0:T(8,128)(2,1)S(1)}, u32[]{:S(2)}, u32[]{:S(2)}) collective-permute-start(bf16[512,384]{1,0:T(8,128)(2,1)} %quant_weight.4), channel_id=1, source_target_pairs={{0,1},{1,0},{2,3},{3,2},{4,5},{5,4},{6,7},{7,6},{8,9},{9,8},{10,11... | collective-permute-start | bytes 1179656 | tf_op jit(solution)/shard_map/ppermute | solution.py:258
  38.7 0.8 copy-start.3
  47.1 61.1 %collective-permute-start.2 = (bf16[512,2048]{1,0:T(8,128)(2,1)}, bf16[512,2048]{1,0:T(8,128)(2,1)}, u32[]{:S(2)}, u32[]{:S(2)}) collective-permute-start(bf16[512,2048]{1,0:T(8,128)(2,1)} %quant_weight.5.refs_3_), channel_id=1, source_target_pairs={{0,1},{1,0},{2,3},{3,2},{4,5},{5,4},{6,7},{7,6},{8,9},{9,8},{10,11... | collective-permute-start | bytes 6291464 | tf_op jit(solution)/shard_map/ppermute | solution.py:261
  49.7 8.5 %copy-start.5 = (bf16[2,2048,128]{2,1,0:T(8,128)(2,1)S(1)}, bf16[2,2048,128]{2,1,0:T(8,128)(2,1)}, u32[]{:S(2)}) copy-start(bf16[2,2048,128]{2,1,0:T(8,128)(2,1)} %all-gather.5.cloned.1.call-done) | copy-start | bytes 3145732
  58.3 5.7 %copy-start.6 = (u32[32]{0:T(128)S(1)}, u32[32]{0:T(128)}, u32[]{:S(2)}) copy-start(u32[32]{0:T(128)} %constant.43) | copy-start | bytes 388
  58.3 28.0 %copy-start.4 = (bf16[8192]{0:T(1024)(128)(2,1)S(1)}, bf16[8192]{0:T(1024)(128)(2,1)}, u32[]{:S(2)}) copy-start(bf16[8192]{0:T(1024)(128)(2,1)} %param.11) | copy-start | bytes 49156
  63.7 44.4 %collective-permute-start = (bf16[512,256]{1,0:T(8,128)(2,1)S(1)}, bf16[512,256]{1,0:T(8,128)(2,1)S(1)}, u32[]{:S(2)}, u32[]{:S(2)}) collective-permute-start(bf16[512,256]{1,0:T(8,128)(2,1)S(1)} %get-tuple-element.18), channel_id=1, source_target_pairs={{0,1},{1,0},{2,3},{3,2},{4,5},{5,4},{6,7},{7,6},{8,9},{9,8},{10,11... | collective-permute-start | bytes 786440 | tf_op jit(solution)/shard_map/ppermute | solution.py:271
  108.2 0.8 copy-start.2
  117.4 56.0 %copy-start.1 = (bf16[512,512]{1,0:T(8,128)(2,1)S(1)}, bf16[512,512]{1,0:T(8,128)(2,1)}, u32[]{:S(2)}) copy-start(bf16[512,512]{1,0:T(8,128)(2,1)} %param.6) | copy-start | bytes 1572868
Sparse Core Ops, SparseCore 0:
  9.6 19.4 all-gather.4
  39.7 63.3 all-gather.6
